TPU v7x, 32 devices: a whole 2x2x4 slice. The times are simulated.
32 devices in a mesh: filt: 4 (over y, x), dom: 8 (over z, core).
Axes of the slice: x: 2, y: 2, z: 4, core: 2. Of those that a mesh axis runs over, the one named last changes fastest.
Arguments:
- log_weights: float32 [524288], P(('filt', 'dom')), parts along dimension 0, may hold values from -20 to 250, as said below
- bins: int32 [524288], P(('filt', 'dom')), parts along dimension 0, may hold values from 0 to 4095
- states: bfloat16 [128, 524288], P(None, ('filt', 'dom')), parts along dimension 1, may hold values from -6 to 6
Outputs:
- cumulative: float32 [16384], P(('filt', 'dom')), parts along dimension 0
- bin_means: float32 [128, 16384], P(None, ('filt', 'dom')), parts along dimension 1
- particle_weights: float32 [524288], P(('filt', 'dom')), parts along dimension 0
There are 4 independent parts, one for each index of `filt`. A program takes and returns all parts, laid end to end along the dimension named above; each array names one. Nothing has to cross between parts.
Inputs may be any that keep to these rules, and one draw needn't show every extreme that they name: `log_weights`: finite log-weights.
All inputs are finite; a program needn't handle non-finite values.
Results may differ from a plain program's by a relative error of at most 0.00051.
Values sent between devices are 32-bit elements; how exact they have to be, the bound alone decides.
A program may use at most 64 MiB of HBM per device.

v0:
```python
import jax
import jax.numpy as jnp
from jax import lax
from jax.sharding import PartitionSpec as P

BINS = 4096


floor_value = -10000.0


def local_pairs(log_weights, bins, states):
    count = log_weights.shape[0]
    width = min(count, 1024)
    blocks = count // width
    labels = lax.iota(jnp.int32, BINS)

    def top_step(index, carry):
        start = index * width
        row_weights = lax.dynamic_slice_in_dim(log_weights, start, width)
        row_bins = lax.dynamic_slice_in_dim(bins, start, width)
        member = row_bins[:, None] == labels[None, :]
        return jnp.maximum(
            carry, jnp.max(jnp.where(member, row_weights[:, None], floor_value), axis=0)
        )

    bin_top = lax.fori_loop(0, blocks, top_step, jnp.full((BINS,), floor_value, jnp.float32))
    ones_row = jnp.ones((1, width), jnp.bfloat16)

    def sum_step(index, carry):
        totals, sums = carry
        start = index * width
        row_weights = lax.dynamic_slice_in_dim(log_weights, start, width)
        row_bins = lax.dynamic_slice_in_dim(bins, start, width)
        row_states = lax.dynamic_slice_in_dim(states, start, width, 1)
        member = row_bins[:, None] == labels[None, :]
        own_top = jnp.take(bin_top, row_bins)
        scaled = jnp.exp(row_weights - own_top).astype(jnp.bfloat16)
        spread = jnp.where(member, scaled[:, None], jnp.zeros((), jnp.bfloat16))
        totals = totals + jnp.dot(ones_row, spread, preferred_element_type=jnp.float32)[0]
        sums = sums + jnp.dot(row_states, spread, preferred_element_type=jnp.float32)
        return (totals, sums)

    start_pair = (jnp.zeros((BINS,), jnp.float32), jnp.zeros((states.shape[0], BINS), jnp.float32))
    totals, sums = lax.fori_loop(0, blocks, sum_step, start_pair)
    return (bin_top, totals, sums)


def body(log_weights, bins, states):
    groups = lax.axis_size("dom")
    owned = BINS // groups
    bin_top, totals, sums = local_pairs(log_weights, bins, states)
    top_pieces, mass_pieces, sum_pieces = (
        lax.all_to_all(bin_top[None, :], "dom", split_axis=1, concat_axis=0, tiled=True),
        lax.all_to_all(totals[None, :], "dom", split_axis=1, concat_axis=0, tiled=True),
        lax.all_to_all(sums, "dom", split_axis=1, concat_axis=0, tiled=True),
    )
    sum_pieces = sum_pieces.reshape(groups, sums.shape[0], owned)
    owned_top = jnp.max(top_pieces, axis=0)
    factor = jnp.exp(top_pieces - owned_top[None, :])
    owned_mass = jnp.sum(mass_pieces * factor, axis=0)
    owned_sums = jnp.sum(sum_pieces * factor[:, None, :], axis=0)
    block_top = jnp.max(owned_top)
    block_mass = jnp.sum(owned_mass * jnp.exp(owned_top - block_top))
    share = None
    all_tops, all_masses = (
        lax.all_gather(block_top[None], "dom", axis=0, tiled=True),
        lax.all_gather(block_mass[None], "dom", axis=0, tiled=True),
    )
    top = jnp.max(all_tops)
    scaled_masses = all_masses * jnp.exp(all_tops - top)
    total = jnp.sum(scaled_masses)
    lower = lax.iota(jnp.int32, groups) < lax.axis_index("dom")
    before = jnp.sum(jnp.where(lower, scaled_masses, jnp.float32(0.0)))
    share = owned_mass * jnp.exp(owned_top - top)
    cumulative = (before + jnp.cumsum(share)) / total
    bin_means = owned_sums / jnp.maximum(owned_mass, 1.0)[None, :]
    whole_count = log_weights.shape[0] * groups
    particle_weights = whole_count * jnp.exp(log_weights - top) / total
    return (cumulative, bin_means, particle_weights)


def solution(mesh):
    placed = (P(("filt", "dom")), P(("filt", "dom")), P(None, ("filt", "dom")))
    return jax.shard_map(
        body,
        mesh=mesh,
        in_specs=placed,
        out_specs=(P(("filt", "dom")), P(None, ("filt", "dom")), P(("filt", "dom"))),
        check_vma=False,
    )
```

profile of v0, /device:TPU:16, one launch (start us, length us, event | category | flops | bytes accessed | tf_op | source)
XLA Modules:
  0.0 426.6 jit_solution(2774227915894027534)
XLA Ops:
  0.7 152.2 %while.30 = (s32[]{:T(128)}, f32[4096]{0:T(1024)}, s32[16384]{0:T(1024)}, f32[16384]{0:T(1024)}, s32[]{:T(128)}, /*index=5*/s32[]{:T(128)}, s32[]{:T(128)}, s32[]{:T(128)}) while((s32[]{:T(128)}, f32[4096]{0:T(1024)}, s32[16384]{0:T(1024)}, f32[16384]{0:T(1024)}, s32[]{:T(128)}, /*index=5*/s32[]{:T(128)}, s32[]{:T(128)}, ...), condition=%wide.region_2.3_spmd.clone, body=%wide.region_0.2_spmd.clone.sunk | while | flops 12587015 | bytes 90269 | solution.py:27
  2.1 6.8 %select_reduce_fusion.2 = f32[4096]{0:T(1024)S(1)} fusion(f32[1024]{0:T(1024)S(1)} %dynamic_slice.49, s32[1024]{0:T(1024)S(1)} %dynamic_slice.50), kind=kLoop, calls=%fused_computation.4.clone.1 | loop fusion | flops 12578816 | bytes 24576 | tf_op jit(solution)/shard_map/while/body/eval_jaxpr/reduce_max | solution.py:24
  10.9 6.8 %select_reduce_fusion.2 = f32[4096]{0:T(1024)S(1)} fusion(f32[1024]{0:T(1024)S(1)} %dynamic_slice.49, s32[1024]{0:T(1024)S(1)} %dynamic_slice.50), kind=kLoop, calls=%fused_computation.4.clone.1 | loop fusion | flops 12578816 | bytes 24576 | tf_op jit(solution)/shard_map/while/body/eval_jaxpr/reduce_max | solution.py:24
  20.4 6.8 %select_reduce_fusion.2 = f32[4096]{0:T(1024)S(1)} fusion(f32[1024]{0:T(1024)S(1)} %dynamic_slice.49, s32[1024]{0:T(1024)S(1)} %dynamic_slice.50), kind=kLoop, calls=%fused_computation.4.clone.1 | loop fusion | flops 12578816 | bytes 24576 | tf_op jit(solution)/shard_map/while/body/eval_jaxpr/reduce_max | solution.py:24
  30.0 6.8 %select_reduce_fusion.2 = f32[4096]{0:T(1024)S(1)} fusion(f32[1024]{0:T(1024)S(1)} %dynamic_slice.49, s32[1024]{0:T(1024)S(1)} %dynamic_slice.50), kind=kLoop, calls=%fused_computation.4.clone.1 | loop fusion | flops 12578816 | bytes 24576 | tf_op jit(solution)/shard_map/while/body/eval_jaxpr/reduce_max | solution.py:24
  39.6 6.8 %select_reduce_fusion.2 = f32[4096]{0:T(1024)S(1)} fusion(f32[1024]{0:T(1024)S(1)} %dynamic_slice.49, s32[1024]{0:T(1024)S(1)} %dynamic_slice.50), kind=kLoop, calls=%fused_computation.4.clone.1 | loop fusion | flops 12578816 | bytes 24576 | tf_op jit(solution)/shard_map/while/body/eval_jaxpr/reduce_max | solution.py:24
  49.1 6.8 %select_reduce_fusion.2 = f32[4096]{0:T(1024)S(1)} fusion(f32[1024]{0:T(1024)S(1)} %dynamic_slice.49, s32[1024]{0:T(1024)S(1)} %dynamic_slice.50), kind=kLoop, calls=%fused_computation.4.clone.1 | loop fusion | flops 12578816 | bytes 24576 | tf_op jit(solution)/shard_map/while/body/eval_jaxpr/reduce_max | solution.py:24
  58.7 6.8 %select_reduce_fusion.2 = f32[4096]{0:T(1024)S(1)} fusion(f32[1024]{0:T(1024)S(1)} %dynamic_slice.49, s32[1024]{0:T(1024)S(1)} %dynamic_slice.50), kind=kLoop, calls=%fused_computation.4.clone.1 | loop fusion | flops 12578816 | bytes 24576 | tf_op jit(solution)/shard_map/while/body/eval_jaxpr/reduce_max | solution.py:24
  68.2 6.8 %select_reduce_fusion.2 = f32[4096]{0:T(1024)S(1)} fusion(f32[1024]{0:T(1024)S(1)} %dynamic_slice.49, s32[1024]{0:T(1024)S(1)} %dynamic_slice.50), kind=kLoop, calls=%fused_computation.4.clone.1 | loop fusion | flops 12578816 | bytes 24576 | tf_op jit(solution)/shard_map/while/body/eval_jaxpr/reduce_max | solution.py:24
  77.8 6.8 %select_reduce_fusion.2 = f32[4096]{0:T(1024)S(1)} fusion(f32[1024]{0:T(1024)S(1)} %dynamic_slice.49, s32[1024]{0:T(1024)S(1)} %dynamic_slice.50), kind=kLoop, calls=%fused_computation.4.clone.1 | loop fusion | flops 12578816 | bytes 24576 | tf_op jit(solution)/shard_map/while/body/eval_jaxpr/reduce_max | solution.py:24
  87.3 6.8 %select_reduce_fusion.2 = f32[4096]{0:T(1024)S(1)} fusion(f32[1024]{0:T(1024)S(1)} %dynamic_slice.49, s32[1024]{0:T(1024)S(1)} %dynamic_slice.50), kind=kLoop, calls=%fused_computation.4.clone.1 | loop fusion | flops 12578816 | bytes 24576 | tf_op jit(solution)/shard_map/while/body/eval_jaxpr/reduce_max | solution.py:24
  96.9 6.8 %select_reduce_fusion.2 = f32[4096]{0:T(1024)S(1)} fusion(f32[1024]{0:T(1024)S(1)} %dynamic_slice.49, s32[1024]{0:T(1024)S(1)} %dynamic_slice.50), kind=kLoop, calls=%fused_computation.4.clone.1 | loop fusion | flops 12578816 | bytes 24576 | tf_op jit(solution)/shard_map/while/body/eval_jaxpr/reduce_max | solution.py:24
  106.4 6.8 %select_reduce_fusion.2 = f32[4096]{0:T(1024)S(1)} fusion(f32[1024]{0:T(1024)S(1)} %dynamic_slice.49, s32[1024]{0:T(1024)S(1)} %dynamic_slice.50), kind=kLoop, calls=%fused_computation.4.clone.1 | loop fusion | flops 12578816 | bytes 24576 | tf_op jit(solution)/shard_map/while/body/eval_jaxpr/reduce_max | solution.py:24
  116.0 6.8 %select_reduce_fusion.2 = f32[4096]{0:T(1024)S(1)} fusion(f32[1024]{0:T(1024)S(1)} %dynamic_slice.49, s32[1024]{0:T(1024)S(1)} %dynamic_slice.50), kind=kLoop, calls=%fused_computation.4.clone.1 | loop fusion | flops 12578816 | bytes 24576 | tf_op jit(solution)/shard_map/while/body/eval_jaxpr/reduce_max | solution.py:24
  125.5 6.8 %select_reduce_fusion.2 = f32[4096]{0:T(1024)S(1)} fusion(f32[1024]{0:T(1024)S(1)} %dynamic_slice.49, s32[1024]{0:T(1024)S(1)} %dynamic_slice.50), kind=kLoop, calls=%fused_computation.4.clone.1 | loop fusion | flops 12578816 | bytes 24576 | tf_op jit(solution)/shard_map/while/body/eval_jaxpr/reduce_max | solution.py:24
  135.1 6.8 %select_reduce_fusion.2 = f32[4096]{0:T(1024)S(1)} fusion(f32[1024]{0:T(1024)S(1)} %dynamic_slice.49, s32[1024]{0:T(1024)S(1)} %dynamic_slice.50), kind=kLoop, calls=%fused_computation.4.clone.1 | loop fusion | flops 12578816 | bytes 24576 | tf_op jit(solution)/shard_map/while/body/eval_jaxpr/reduce_max | solution.py:24
  144.6 6.8 %select_reduce_fusion.2 = f32[4096]{0:T(1024)S(1)} fusion(f32[1024]{0:T(1024)S(1)} %dynamic_slice.49, s32[1024]{0:T(1024)S(1)} %dynamic_slice.50), kind=kLoop, calls=%fused_computation.4.clone.1 | loop fusion | flops 12578816 | bytes 24576 | tf_op jit(solution)/shard_map/while/body/eval_jaxpr/reduce_max | solution.py:24
  152.8 189.3 %while.31 = (s32[]{:T(128)}, f32[4096]{0:T(1024)S(1)}, f32[128,4096]{1,0:T(8,128)S(1)}, s32[16384]{0:T(1024)}, f32[16384]{0:T(1024)}, /*index=5*/f32[4096]{0:T(1...) while((s32[]{:T(128)}, f32[4096]{0:T(1024)S(1)}, ...), condition=%wide.region_4.5_spmd.clone, body=%wide.region_3.4_spmd.clone.sunk | while | flops 1099977728 | bytes 4573370 | solution.py:45
  153.5 5.7 %gather_fusion = f32[1024]{0:T(1024)S(1)} fusion(f32[4096]{0:T(1024)} %get-tuple-element.440, s32[1024]{0:T(1024)S(1)} %get-tuple-element.388), kind=kCustom, calls=%fused_computation.clone.clone.1 | custom fusion | bytes 12288 | tf_op jit(solution)/shard_map/while/body/eval_jaxpr/jit(_take)/gather | solution.py:37
  165.3 5.7 %gather_fusion = f32[1024]{0:T(1024)S(1)} fusion(f32[4096]{0:T(1024)} %get-tuple-element.440, s32[1024]{0:T(1024)S(1)} %get-tuple-element.388), kind=kCustom, calls=%fused_computation.clone.clone.1 | custom fusion | bytes 12288 | tf_op jit(solution)/shard_map/while/body/eval_jaxpr/jit(_take)/gather | solution.py:37
  177.2 5.7 %gather_fusion = f32[1024]{0:T(1024)S(1)} fusion(f32[4096]{0:T(1024)} %get-tuple-element.440, s32[1024]{0:T(1024)S(1)} %get-tuple-element.388), kind=kCustom, calls=%fused_computation.clone.clone.1 | custom fusion | bytes 12288 | tf_op jit(solution)/shard_map/while/body/eval_jaxpr/jit(_take)/gather | solution.py:37
  189.0 5.7 %gather_fusion = f32[1024]{0:T(1024)S(1)} fusion(f32[4096]{0:T(1024)} %get-tuple-element.440, s32[1024]{0:T(1024)S(1)} %get-tuple-element.388), kind=kCustom, calls=%fused_computation.clone.clone.1 | custom fusion | bytes 12288 | tf_op jit(solution)/shard_map/while/body/eval_jaxpr/jit(_take)/gather | solution.py:37
  200.8 5.7 %gather_fusion = f32[1024]{0:T(1024)S(1)} fusion(f32[4096]{0:T(1024)} %get-tuple-element.440, s32[1024]{0:T(1024)S(1)} %get-tuple-element.388), kind=kCustom, calls=%fused_computation.clone.clone.1 | custom fusion | bytes 12288 | tf_op jit(solution)/shard_map/while/body/eval_jaxpr/jit(_take)/gather | solution.py:37
  212.7 5.7 %gather_fusion = f32[1024]{0:T(1024)S(1)} fusion(f32[4096]{0:T(1024)} %get-tuple-element.440, s32[1024]{0:T(1024)S(1)} %get-tuple-element.388), kind=kCustom, calls=%fused_computation.clone.clone.1 | custom fusion | bytes 12288 | tf_op jit(solution)/shard_map/while/body/eval_jaxpr/jit(_take)/gather | solution.py:37
  224.5 5.7 %gather_fusion = f32[1024]{0:T(1024)S(1)} fusion(f32[4096]{0:T(1024)} %get-tuple-element.440, s32[1024]{0:T(1024)S(1)} %get-tuple-element.388), kind=kCustom, calls=%fused_computation.clone.clone.1 | custom fusion | bytes 12288 | tf_op jit(solution)/shard_map/while/body/eval_jaxpr/jit(_take)/gather | solution.py:37
  236.3 5.7 %gather_fusion = f32[1024]{0:T(1024)S(1)} fusion(f32[4096]{0:T(1024)} %get-tuple-element.440, s32[1024]{0:T(1024)S(1)} %get-tuple-element.388), kind=kCustom, calls=%fused_computation.clone.clone.1 | custom fusion | bytes 12288 | tf_op jit(solution)/shard_map/while/body/eval_jaxpr/jit(_take)/gather | solution.py:37
  248.2 5.7 %gather_fusion = f32[1024]{0:T(1024)S(1)} fusion(f32[4096]{0:T(1024)} %get-tuple-element.440, s32[1024]{0:T(1024)S(1)} %get-tuple-element.388), kind=kCustom, calls=%fused_computation.clone.clone.1 | custom fusion | bytes 12288 | tf_op jit(solution)/shard_map/while/body/eval_jaxpr/jit(_take)/gather | solution.py:37
  260.0 5.7 %gather_fusion = f32[1024]{0:T(1024)S(1)} fusion(f32[4096]{0:T(1024)} %get-tuple-element.440, s32[1024]{0:T(1024)S(1)} %get-tuple-element.388), kind=kCustom, calls=%fused_computation.clone.clone.1 | custom fusion | bytes 12288 | tf_op jit(solution)/shard_map/while/body/eval_jaxpr/jit(_take)/gather | solution.py:37
  271.8 5.7 %gather_fusion = f32[1024]{0:T(1024)S(1)} fusion(f32[4096]{0:T(1024)} %get-tuple-element.440, s32[1024]{0:T(1024)S(1)} %get-tuple-element.388), kind=kCustom, calls=%fused_computation.clone.clone.1 | custom fusion | bytes 12288 | tf_op jit(solution)/shard_map/while/body/eval_jaxpr/jit(_take)/gather | solution.py:37
  319.2 5.7 %gather_fusion = f32[1024]{0:T(1024)S(1)} fusion(f32[4096]{0:T(1024)} %get-tuple-element.440, s32[1024]{0:T(1024)S(1)} %get-tuple-element.388), kind=kCustom, calls=%fused_computation.clone.clone.1 | custom fusion | bytes 12288 | tf_op jit(solution)/shard_map/while/body/eval_jaxpr/jit(_take)/gather | solution.py:37
  342.1 8.3 %all_to_all.45 = f32[1,8,512]{2,0,1:T(1,128)S(1)} all-to-all(f32[1,8,512]{2,0,1:T(1,128)S(1)} %bitcast.23), channel_id=1, replica_groups=mesh['filt'=4,'dom'=8] {'dom'}, dimensions={1} | all-to-all | bytes 32768 | tf_op jit(solution)/shard_map/all_to_all | solution.py:55
  370.6 48.1 %all-reduce.2 = (f32[8]{0:T(128)S(1)}, f32[8]{0:T(128)S(1)}) all-reduce(f32[8]{0:T(128)S(1)} %dynamic-update-slice.1, f32[8]{0:T(128)S(1)} %dynamic-update-slice), channel_id=1, replica_groups=mesh['filt'=4,'dom'=8] {'dom'}, use_global_device_ids=true, to_apply=%add.1 | all-reduce | flops 16 | bytes 128
  (166 shorter events, 190.4 us)
Async XLA Ops:
  342.1 13.9 %copy-start = (f32[128,4096]{1,0:T(8,128)}, f32[128,4096]{1,0:T(8,128)S(1)}, u32[]{:S(2)}) copy-start(f32[128,4096]{1,0:T(8,128)S(1)} %get-tuple-element.239) | copy-start | bytes 6291460
  350.4 9.5 %all-to-all-start.1 = ((f32[1,8,512]{2,0,1:T(1,128)}), f32[1,8,512]{2,0,1:T(1,128)S(1)}, u32[]{:S(2)}, u32[]{:S(2)}) async-start(f32[1,8,512]{2,0,1:T(1,128)} %bitcast.1), calls=%async_computation.1 | async-start | bytes 32768 | tf_op jit(solution)/shard_map/all_to_all | solution.py:54
  358.0 7.3 %copy-start.2 = (u32[32]{0:T(128)S(1)}, u32[32]{0:T(128)}, u32[]{:S(2)}) copy-start(u32[32]{0:T(128)} %constant.132) | copy-start | bytes 388
  358.0 65.7 %copy-start.1 = (f32[16384]{0:T(1024)S(1)}, f32[16384]{0:T(1024)}, u32[]{:S(2)}) copy-start(f32[16384]{0:T(1024)} %get-tuple-element.448) | copy-start | bytes 196612
  359.9 65.7 %all-to-all-start.2 = ((f32[128,8,512]{2,0,1:T(8,128)}), f32[128,8,512]{2,0,1:T(8,128)S(1)}, u32[]{:S(2)}, u32[]{:S(2)}) async-start(f32[128,8,512]{2,0,1:T(8,128)} %copy.9), calls=%async_computation.2 | async-start | bytes 4194304 | tf_op jit(solution)/shard_map/all_to_all | solution.py:56
where the time goes:
time: 432 us; the launch traced here: 427 us
  other arithmetic  162 us (38%)
  local copies, waits for them, and re-layouts  121 us (28%)
  matrix products  74.2 us (17%)
  blocking collectives  56.4 us (13%)
  starting transfers between devices  11 us (3%)
    reduce_max x16, other arithmetic, top_step(): jnp.max(jnp.where(member, row_weights[:, None], floor_value), axis=0)  109 us
    gather x16, local copies, waits for them, and re-layouts, sum_step(): own_top = jnp.take(bin_top, row_bins)  92 us
    dot_general x16, matrix products, sum_step(): jnp.dot(row_states, spread, preferred_element_type=jnp.float32)  51.7 us
    unnamed x1, blocking collectives  48.1 us
    dot_general x16, matrix products, sum_step(): jnp.dot(ones_row, spread, preferred_element_type=jnp.float32)[0]  22.5 us
    max x16, other arithmetic, top_step(): jnp.maximum(carry, jnp.max(jnp.where(member, row_weights[:, None], floor_...  20.7 us
    convert_element_type x16, other arithmetic, sum_step(): scaled = jnp.exp(row_weights - own_top).astype(jnp.bfloat16)  11.2 us
    gather x16, other arithmetic, sum_step(): own_top = jnp.take(bin_top, row_bins)  11.1 us
  transfers between devices with their start and end apart: 2, of which 0 were waited for; matrix products, arithmetic and copies ran while one was open for 4% of the time, Pallas kernels for 0%

commit v1 on v0

v1 whole, which is shorter than its diff:
```python
import functools

import jax
import jax.numpy as jnp
from jax import lax
from jax.experimental import pallas as pl
from jax.experimental.pallas import tpu as pltpu
from jax.sharding import PartitionSpec as P

BINS = 4096
LANES = 128
EXTRA = 16

floor_value = -10000.0


def spread_rows(ref, values):
    for r in range(values.shape[0]):
        ref[16 * r:16 * r + 16, :] = jnp.broadcast_to(values[r:r + 1, :], (16, LANES)).astype(ref.dtype)


def local_tops(lw_t, bins_t):
    rows = lw_t.shape[1]
    tiles = BINS // LANES
    lane = lax.broadcasted_iota(jnp.int32, (8, LANES), 1)

    def step(r, acc):
        pick = jnp.full((LANES, LANES), r, jnp.int32)
        col_w = jnp.take_along_axis(lw_t, pick, axis=1).reshape(LANES // 8, 8, LANES)
        col_b = jnp.take_along_axis(bins_t, pick, axis=1).reshape(LANES // 8, 8, LANES)
        out = []
        for t in range(tiles):
            member = col_b == (lane + t * LANES)[None]
            out.append(jnp.maximum(acc[t], jnp.max(jnp.where(member, col_w, floor_value), axis=0)))
        return tuple(out)

    start = tuple(jnp.full((8, LANES), floor_value, jnp.float32) for _ in range(tiles))
    acc = lax.fori_loop(0, rows, step, start)
    return [jnp.max(a, axis=0, keepdims=True) for a in acc]


def merge(a, b, state):
    top_a, top_b = a[state + 8:state + 9], b[state + 8:state + 9]
    top = jnp.maximum(top_a, top_b)
    rows = a[0:state + 8] * jnp.exp(top_a - top) + b[0:state + 8] * jnp.exp(top_b - top)
    return rows, jnp.broadcast_to(top, (8, top.shape[1]))


def kernel(groups, whole_count, lw_ref, bins_ref, states_ref, cum_ref, means_ref, weights_ref,
           ext, lo_b, hi_b, w_b, top_tab, mine, pair_send, pair_recv, chip_send, chip_recv,
           stat_send, stat_recv, load_sem, pair_ss, pair_rs, chip_ss, chip_rs, stat_ss, stat_rs):
    state = states_ref.shape[0]
    count = states_ref.shape[1]
    rows = count // LANES
    owned = BINS // groups
    width = min(256, owned)
    chips = groups // 2
    me = lax.axis_index("dom")
    chip, core = me // 2, me % 2
    partner = chip * 2 + (1 - core)

    load = pltpu.make_async_copy(states_ref, ext.at[0:state], load_sem)
    load.start()
    barrier = pltpu.get_barrier_semaphore()
    for k in range(1, groups):
        pl.semaphore_signal(barrier, inc=1, device_id={"dom": lax.rem(me + k, groups)},
                            device_id_type=pl.DeviceIdType.MESH)

    ext[state:state + EXTRA, :] = jnp.ones((EXTRA, count), jnp.bfloat16)
    lw = lw_ref[...]
    bins = bins_ref[...]
    spread_rows(lo_b, (bins % width).astype(jnp.float32))
    spread_rows(hi_b, (bins // width).astype(jnp.float32))
    tops = local_tops(lw.T, bins.T)
    low, high = bins % LANES, bins // LANES
    own_top = jnp.zeros(lw.shape, jnp.float32)
    for t in range(BINS // LANES):
        picked = jnp.take_along_axis(jnp.broadcast_to(tops[t], lw.shape), low, axis=1)
        own_top = jnp.where(high == t, picked, own_top)
        top_tab[t] = jnp.broadcast_to(tops[t], (8, LANES))
    spread_rows(w_b, jnp.exp(lw - own_top))
    load.wait()
    pl.semaphore_wait(barrier, groups - 1)

    depth = 16
    label = lax.broadcasted_iota(jnp.int32, (width, LANES), 0).astype(jnp.float32).astype(jnp.bfloat16)
    zero = jnp.zeros((), jnp.bfloat16)

    def block(owner, out):
        for part in range(owned // width):
            tile = (owner * (owned // width) + part).astype(jnp.float32).astype(jnp.bfloat16)

            def step(c, acc):
                pieces = []
                for j in range(depth):
                    at = pl.ds(pl.multiple_of((c * depth + j) * 16, 16), 16)
                    w = jnp.where(hi_b[at, :] == tile, w_b[at, :], zero)
                    lo = lo_b[at, :]
                    w_all = jnp.concatenate([w] * (width // 16), axis=0)
                    lo_all = jnp.concatenate([lo] * (width // 16), axis=0)
                    pieces.append(jnp.where(lo_all == label, w_all, zero))
                spread = jnp.concatenate(pieces, axis=1)
                cols = pl.ds(pl.multiple_of(c * depth * LANES, LANES), depth * LANES)
                return acc + lax.dot_general(ext[:, cols], spread, (((1,), (1,)), ((), ())),
                                             preferred_element_type=jnp.float32)

            acc = lax.fori_loop(0, rows // depth, step, jnp.zeros((state + EXTRA, width), jnp.float32))
            out[:, part * width:(part + 1) * width] = acc
        for t in range(owned // LANES):
            out[state + 8:state + 16, t * LANES:(t + 1) * LANES] = top_tab[owner * (owned // LANES) + t]

    order = sorted(range(1, chips), key=lambda m: -min(m, chips - m)) + [0]
    pair_copies, chip_copies = [], []
    for s, m in enumerate(order):
        dest = lax.rem(chip + m, chips)
        block(dest * 2 + (1 - core), pair_send.at[s])
        copy = pltpu.make_async_remote_copy(
            pair_send.at[s], pair_recv.at[s], pair_ss.at[s], pair_rs.at[s],
            device_id={"dom": partner}, device_id_type=pl.DeviceIdType.MESH)
        copy.start()
        pair_copies.append(copy)
        block(dest * 2 + core, mine.at[s])
        copy.wait_recv()
        merged, top = merge(mine[s], pair_recv[s], state)
        chip_send[s, 0:state + 8, :] = merged
        chip_send[s, state + 8:state + 16, :] = top
        if m:
            copy = pltpu.make_async_remote_copy(
                chip_send.at[s], chip_recv.at[s], chip_ss.at[s], chip_rs.at[s],
                device_id={"dom": dest * 2 + core}, device_id_type=pl.DeviceIdType.MESH)
            copy.start()
            chip_copies.append(copy)

    for copy in chip_copies:
        copy.wait_recv()
    last = chips - 1
    tops = [chip_send[last, state + 8:state + 9, :]] + [chip_recv[s, state + 8:state + 9, :] for s in range(last)]
    bin_top = functools.reduce(jnp.maximum, tops)
    sums = chip_send[last, 0:state + 8, :] * jnp.exp(tops[0] - bin_top)
    for s in range(last):
        sums = sums + chip_recv[s, 0:state + 8, :] * jnp.exp(tops[s + 1] - bin_top)
    mass = sums[state:state + 1, :]
    block_top = jnp.max(bin_top, axis=1, keepdims=True)
    block_mass = jnp.sum(mass * jnp.exp(bin_top - block_top), axis=1, keepdims=True)
    stat_send[0:4, :] = jnp.broadcast_to(block_top, (4, LANES))
    stat_send[4:8, :] = jnp.broadcast_to(block_mass, (4, LANES))
    stat_copies = []
    for k in range(1, groups):
        copy = pltpu.make_async_remote_copy(
            stat_send, stat_recv.at[k - 1], stat_ss.at[k - 1], stat_rs.at[k - 1],
            device_id={"dom": lax.rem(me + k, groups)}, device_id_type=pl.DeviceIdType.MESH)
        copy.start()
        stat_copies.append(copy)
    means_ref[...] = sums[0:state] / jnp.maximum(mass, 1.0)
    for copy in stat_copies:
        copy.wait_recv()
    top = block_top
    for k in range(groups - 1):
        top = jnp.maximum(top, stat_recv[k, 0:1, 0:1])
    total = block_mass * jnp.exp(block_top - top)
    before = jnp.zeros_like(total)
    for k in range(groups - 1):
        theirs = stat_recv[k, 4:5, 0:1] * jnp.exp(stat_recv[k, 0:1, 0:1] - top)
        total = total + theirs
        before = before + jnp.where(me >= k + 1, theirs, 0.0)
    share = mass * jnp.exp(bin_top - top)
    position = lax.broadcasted_iota(jnp.int32, share.shape, 1)
    run = share
    hop = 1
    while hop < owned:
        run = run + jnp.where(position >= hop, pltpu.roll(run, hop, 1), 0.0)
        hop *= 2
    cum_ref[...] = (before + run) / total
    weights_ref[...] = whole_count * jnp.exp(lw - top) / total
    for copy in pair_copies + chip_copies + stat_copies:
        copy.wait_send()


def body(log_weights, bins, states):
    groups = lax.axis_size("dom")
    owned = BINS // groups
    chips = groups // 2
    state, count = states.shape
    rows = count // LANES
    vmem = pl.BlockSpec(memory_space=pltpu.VMEM)
    blocks = pltpu.VMEM((chips, state + EXTRA, owned), jnp.float32)
    cumulative, bin_means, weights = pl.pallas_call(
        functools.partial(kernel, groups, float(count * groups)),
        out_shape=(jax.ShapeDtypeStruct((1, owned), jnp.float32),
                   jax.ShapeDtypeStruct((state, owned), jnp.float32),
                   jax.ShapeDtypeStruct((rows, LANES), jnp.float32)),
        in_specs=[vmem, vmem, pl.BlockSpec(memory_space=pl.ANY)],
        out_specs=(vmem, vmem, vmem),
        scratch_shapes=[
            pltpu.VMEM((state + EXTRA, count), jnp.bfloat16),
            pltpu.VMEM((rows * 16, LANES), jnp.bfloat16),
            pltpu.VMEM((rows * 16, LANES), jnp.bfloat16),
            pltpu.VMEM((rows * 16, LANES), jnp.bfloat16),
            pltpu.VMEM((BINS // LANES, 8, LANES), jnp.float32),
            blocks, blocks, blocks, blocks, blocks,
            pltpu.VMEM((8, LANES), jnp.float32),
            pltpu.VMEM((groups - 1, 8, LANES), jnp.float32),
            pltpu.SemaphoreType.DMA,
            pltpu.SemaphoreType.DMA((chips,)),
            pltpu.SemaphoreType.DMA((chips,)),
            pltpu.SemaphoreType.DMA((chips,)),
            pltpu.SemaphoreType.DMA((chips,)),
            pltpu.SemaphoreType.DMA((groups - 1,)),
            pltpu.SemaphoreType.DMA((groups - 1,)),
        ],
        compiler_params=pltpu.CompilerParams(
            collective_id=0, has_side_effects=True, vmem_limit_bytes=48 * 1024 * 1024),
    )(log_weights.reshape(rows, LANES), bins.reshape(rows, LANES), states)
    return cumulative.reshape(owned), bin_means, weights.reshape(count)


def solution(mesh):
    placed = (P(("filt", "dom")), P(("filt", "dom")), P(None, ("filt", "dom")))
    return jax.shard_map(
        body,
        mesh=mesh,
        in_specs=placed,
        out_specs=(P(("filt", "dom")), P(None, ("filt", "dom")), P(("filt", "dom"))),
        check_vma=False,
    )
```

time: 432 us -> 127 us (0.29)
  the two profiles are of different devices: /device:TPU:16 before, /device:TPU:0 now
where the time goes in v1:
time: 127 us
  Pallas kernels  120 us (94%)
  local copies, waits for them, and re-layouts  5.78 us (5%)
    pallas_call x1, Pallas kernels, body(): pl.pallas_call(functools.partial(kernel, groups, float(count * groups)),...  120 us
    unnamed x9, local copies, waits for them, and re-layouts  5.78 us

profile of v1, /device:TPU:0, one launch (start us, length us, event | category | flops | bytes accessed | tf_op | source)
XLA Modules:
  0.0 126.7 jit_solution(837349150781262563)
XLA Ops:
  0.6 0.0 copy-start
  0.6 2.2 %copy-done = bf16[128,16384]{1,0:T(8,128)(2,1)S(1)} copy-done((bf16[128,16384]{1,0:T(8,128)(2,1)S(1)}, bf16[128,16384]{1,0:T(8,128)(2,1)}, u32[]{:S(2)}) %copy-start) | copy-done | bytes 4194328
  2.8 0.0 copy-start.1
  2.8 0.8 copy-done.1
  3.7 0.0 copy-start.2
  3.7 0.8 copy-done.2
  4.5 120.3 %shard_map.58 = (f32[1,512]{1,0:T(1,128)S(1)}, f32[128,512]{1,0:T(8,128)S(1)}, f32[128,128]{1,0:T(8,128)S(1)}) custom-call(f32[128,128]{1,0:T(8,128)S(1)} %bitcast.4, s32[128,128]{1,0:T(8,128)S(1)} %bitcast.5, bf16[128,16384]{1,0:T(8,128)(2,1)S(1)} %copy-done), custom_call_target="tpu_custom_call" | custom-call | tf_op jit(solution)/shard_map/pallas_call | solution.py:187
  124.8 0.6 copy.9
  125.4 0.7 copy.10
  126.1 0.6 copy.11
Async XLA Ops:
  0.6 2.2 %copy-start = (bf16[128,16384]{1,0:T(8,128)(2,1)S(1)}, bf16[128,16384]{1,0:T(8,128)(2,1)}, u32[]{:S(2)}) copy-start(bf16[128,16384]{1,0:T(8,128)(2,1)} %states_ref.1) | copy-start | bytes 12582916
  2.8 0.8 copy-start.1
  3.7 0.8 copy-start.2

commit v2 on v1

--- a/solution.py
+++ b/solution.py
@@ -39,38 +39,33 @@
     return [jnp.max(a, axis=0, keepdims=True) for a in acc]
 
 
-def merge(a, b, state):
-    top_a, top_b = a[state + 8:state + 9], b[state + 8:state + 9]
-    top = jnp.maximum(top_a, top_b)
-    rows = a[0:state + 8] * jnp.exp(top_a - top) + b[0:state + 8] * jnp.exp(top_b - top)
-    return rows, jnp.broadcast_to(top, (8, top.shape[1]))
-
-
 def kernel(groups, whole_count, lw_ref, bins_ref, states_ref, cum_ref, means_ref, weights_ref,
-           ext, lo_b, hi_b, w_b, top_tab, mine, pair_send, pair_recv, chip_send, chip_recv,
+           held, ext, lo_b, hi_b, part_b, w_b, top_tab, blocks, pair_send, pair_recv, chip_send, chip_recv,
            stat_send, stat_recv, load_sem, pair_ss, pair_rs, chip_ss, chip_rs, stat_ss, stat_rs):
     state = states_ref.shape[0]
     count = states_ref.shape[1]
     rows = count // LANES
     owned = BINS // groups
+    both = 2 * owned
     width = min(256, owned)
+    split = both // width
     chips = groups // 2
     me = lax.axis_index("dom")
     chip, core = me // 2, me % 2
     partner = chip * 2 + (1 - core)
 
-    load = pltpu.make_async_copy(states_ref, ext.at[0:state], load_sem)
+    load = pltpu.make_async_copy(states_ref, held, load_sem)
     load.start()
     barrier = pltpu.get_barrier_semaphore()
     for k in range(1, groups):
         pl.semaphore_signal(barrier, inc=1, device_id={"dom": lax.rem(me + k, groups)},
                             device_id_type=pl.DeviceIdType.MESH)
 
-    ext[state:state + EXTRA, :] = jnp.ones((EXTRA, count), jnp.bfloat16)
     lw = lw_ref[...]
     bins = bins_ref[...]
     spread_rows(lo_b, (bins % width).astype(jnp.float32))
-    spread_rows(hi_b, (bins // width).astype(jnp.float32))
+    spread_rows(hi_b, (bins // both).astype(jnp.float32))
+    spread_rows(part_b, ((bins % both) // width).astype(jnp.float32))
     tops = local_tops(lw.T, bins.T)
     low, high = bins % LANES, bins // LANES
     own_top = jnp.zeros(lw.shape, jnp.float32)
@@ -80,50 +75,89 @@
         top_tab[t] = jnp.broadcast_to(tops[t], (8, LANES))
     spread_rows(w_b, jnp.exp(lw - own_top))
     load.wait()
+
+    zero = jnp.zeros((), jnp.bfloat16)
+    one_label = lax.broadcasted_iota(jnp.int32, (EXTRA, LANES), 0) // (EXTRA // split)
+    one_label = one_label.astype(jnp.float32).astype(jnp.bfloat16)
+
+    def mask_states(r, carry):
+        part = part_b[pl.ds(pl.multiple_of(r * 16, 16), 16), :]
+        cols = pl.ds(pl.multiple_of(r * LANES, LANES), LANES)
+        tile = held[:, cols]
+        part_all = jnp.concatenate([part] * (state // 16), axis=0)
+        for q in range(split):
+            ext[q * state:(q + 1) * state, cols] = jnp.where(part_all == jnp.bfloat16(q), tile, zero)
+        ext[split * state:split * state + EXTRA, cols] = jnp.where(part == one_label, jnp.bfloat16(1), zero)
+        return carry
+
+    lax.fori_loop(0, rows, mask_states, 0)
     pl.semaphore_wait(barrier, groups - 1)
 
     depth = 16
     label = lax.broadcasted_iota(jnp.int32, (width, LANES), 0).astype(jnp.float32).astype(jnp.bfloat16)
-    zero = jnp.zeros((), jnp.bfloat16)
-
-    def block(owner, out):
-        for part in range(owned // width):
-            tile = (owner * (owned // width) + part).astype(jnp.float32).astype(jnp.bfloat16)
-
-            def step(c, acc):
-                pieces = []
-                for j in range(depth):
-                    at = pl.ds(pl.multiple_of((c * depth + j) * 16, 16), 16)
-                    w = jnp.where(hi_b[at, :] == tile, w_b[at, :], zero)
-                    lo = lo_b[at, :]
-                    w_all = jnp.concatenate([w] * (width // 16), axis=0)
-                    lo_all = jnp.concatenate([lo] * (width // 16), axis=0)
-                    pieces.append(jnp.where(lo_all == label, w_all, zero))
-                spread = jnp.concatenate(pieces, axis=1)
-                cols = pl.ds(pl.multiple_of(c * depth * LANES, LANES), depth * LANES)
-                return acc + lax.dot_general(ext[:, cols], spread, (((1,), (1,)), ((), ())),
-                                             preferred_element_type=jnp.float32)
-
-            acc = lax.fori_loop(0, rows // depth, step, jnp.zeros((state + EXTRA, width), jnp.float32))
-            out[:, part * width:(part + 1) * width] = acc
-        for t in range(owned // LANES):
-            out[state + 8:state + 16, t * LANES:(t + 1) * LANES] = top_tab[owner * (owned // LANES) + t]
+
+    def block(dest, out):
+        tile = dest.astype(jnp.float32).astype(jnp.bfloat16)
+
+        def step(c, carry):
+            pieces = []
+            for j in range(depth):
+                at = pl.ds(pl.multiple_of((c * depth + j) * 16, 16), 16)
+                w = jnp.where(hi_b[at, :] == tile, w_b[at, :], zero)
+                lo = lo_b[at, :]
+                w_all = jnp.concatenate([w] * (width // 16), axis=0)
+                lo_all = jnp.concatenate([lo] * (width // 16), axis=0)
+                pieces.append(jnp.where(lo_all == label, w_all, zero))
+            spread = jnp.concatenate(pieces, axis=1)
+            cols = pl.ds(pl.multiple_of(c * depth * LANES, LANES), depth * LANES)
+            out[...] += lax.dot_general(ext[:, cols], spread, (((1,), (1,)), ((), ())),
+                                        preferred_element_type=jnp.float32)
+            return carry
+
+        out[...] = jnp.zeros(out.shape, jnp.float32)
+        lax.fori_loop(0, rows // depth, step, 0)
+
+    half = split // 2
+
+    def part_of(found, which, p):
+        sums = found[pl.ds(pl.multiple_of((which * half + p) * state, state), state), :]
+        at = split * state + p * (EXTRA // split)
+        first = found[at:at + 1, :]
+        at = at + half * (EXTRA // split)
+        return sums, jnp.where(which == 0, first, found[at:at + 1, :])
+
+    def tops_of(owner, p):
+        tiles = [top_tab[(owner * half + p) * (width // LANES) + t] for t in range(width // LANES)]
+        return jnp.concatenate(tiles, axis=1)
 
     order = sorted(range(1, chips), key=lambda m: -min(m, chips - m)) + [0]
     pair_copies, chip_copies = [], []
     for s, m in enumerate(order):
         dest = lax.rem(chip + m, chips)
-        block(dest * 2 + (1 - core), pair_send.at[s])
+        found = blocks.at[s]
+        block(dest, found)
+        for p in range(half):
+            lanes = slice(p * width, (p + 1) * width)
+            sums, mass = part_of(found, 1 - core, p)
+            pair_send[s, 0:state, lanes] = sums
+            pair_send[s, state:state + 8, lanes] = jnp.broadcast_to(mass, (8, width))
+            pair_send[s, state + 8:state + 16, lanes] = tops_of(dest * 2 + 1 - core, p)
         copy = pltpu.make_async_remote_copy(
             pair_send.at[s], pair_recv.at[s], pair_ss.at[s], pair_rs.at[s],
             device_id={"dom": partner}, device_id_type=pl.DeviceIdType.MESH)
         copy.start()
         pair_copies.append(copy)
-        block(dest * 2 + core, mine.at[s])
         copy.wait_recv()
-        merged, top = merge(mine[s], pair_recv[s], state)
-        chip_send[s, 0:state + 8, :] = merged
-        chip_send[s, state + 8:state + 16, :] = top
+        for p in range(half):
+            lanes = slice(p * width, (p + 1) * width)
+            sums, mass = part_of(found, core, p)
+            mine = tops_of(dest * 2 + core, p)
+            theirs = pair_recv[s, state + 8:state + 16, lanes]
+            top = jnp.maximum(mine, theirs)
+            by_mine, by_theirs = jnp.exp(mine - top), jnp.exp(theirs - top)
+            chip_send[s, 0:state, lanes] = sums * by_mine[0:1] + pair_recv[s, 0:state, lanes] * by_theirs[0:1]
+            chip_send[s, state:state + 8, lanes] = mass * by_mine + pair_recv[s, state:state + 8, lanes] * by_theirs
+            chip_send[s, state + 8:state + 16, lanes] = top
         if m:
             copy = pltpu.make_async_remote_copy(
                 chip_send.at[s], chip_recv.at[s], chip_ss.at[s], chip_rs.at[s],
@@ -182,6 +216,8 @@
     chips = groups // 2
     state, count = states.shape
     rows = count // LANES
+    width = min(256, owned)
+    split = 2 * owned // width
     vmem = pl.BlockSpec(memory_space=pltpu.VMEM)
     blocks = pltpu.VMEM((chips, state + EXTRA, owned), jnp.float32)
     cumulative, bin_means, weights = pl.pallas_call(
@@ -192,12 +228,15 @@
         in_specs=[vmem, vmem, pl.BlockSpec(memory_space=pl.ANY)],
         out_specs=(vmem, vmem, vmem),
         scratch_shapes=[
-            pltpu.VMEM((state + EXTRA, count), jnp.bfloat16),
+            pltpu.VMEM((state, count), jnp.bfloat16),
+            pltpu.VMEM((split * state + EXTRA, count), jnp.bfloat16),
+            pltpu.VMEM((rows * 16, LANES), jnp.bfloat16),
             pltpu.VMEM((rows * 16, LANES), jnp.bfloat16),
             pltpu.VMEM((rows * 16, LANES), jnp.bfloat16),
             pltpu.VMEM((rows * 16, LANES), jnp.bfloat16),
             pltpu.VMEM((BINS // LANES, 8, LANES), jnp.float32),
-            blocks, blocks, blocks, blocks, blocks,
+            pltpu.VMEM((chips, split * state + EXTRA, width), jnp.float32),
+            blocks, blocks, blocks, blocks,
             pltpu.VMEM((8, LANES), jnp.float32),
             pltpu.VMEM((groups - 1, 8, LANES), jnp.float32),
             pltpu.SemaphoreType.DMA,

time: 127 us -> 102 us (0.80)
  Pallas kernels: 120 us -> 95.5 us
    pallas_call x1, Pallas kernels: 120 us -> 95.5 us  [body(): pl.pallas_call(functools.partial(kernel, groups, float(count * groups)),...]
where the time goes in v2:
time: 102 us
  Pallas kernels  95.5 us (94%)
  local copies, waits for them, and re-layouts  5.78 us (6%)
    pallas_call x1, Pallas kernels, body(): pl.pallas_call(functools.partial(kernel, groups, float(count * groups)),...  95.5 us
    unnamed x9, local copies, waits for them, and re-layouts  5.78 us

profile of v2, /device:TPU:0, one launch (start us, length us, event | category | flops | bytes accessed | tf_op | source)
XLA Modules:
  0.0 101.9 jit_solution(10141186682581682922)
XLA Ops:
  0.6 0.0 copy-start
  0.6 2.2 %copy-done = bf16[128,16384]{1,0:T(8,128)(2,1)S(1)} copy-done((bf16[128,16384]{1,0:T(8,128)(2,1)S(1)}, bf16[128,16384]{1,0:T(8,128)(2,1)}, u32[]{:S(2)}) %copy-start) | copy-done | bytes 4194328
  2.8 0.0 copy-start.1
  2.8 0.8 copy-done.1
  3.7 0.0 copy-start.2
  3.7 0.8 copy-done.2
  4.5 95.5 %shard_map.58 = (f32[1,512]{1,0:T(1,128)S(1)}, f32[128,512]{1,0:T(8,128)S(1)}, f32[128,128]{1,0:T(8,128)S(1)}) custom-call(f32[128,128]{1,0:T(8,128)S(1)} %bitcast.4, s32[128,128]{1,0:T(8,128)S(1)} %bitcast.5, bf16[128,16384]{1,0:T(8,128)(2,1)S(1)} %copy-done), custom_call_target="tpu_custom_call" | custom-call | tf_op jit(solution)/shard_map/pallas_call | solution.py:223
  100.0 0.6 copy.9
  100.6 0.7 copy.10
  101.3 0.6 copy.11
Async XLA Ops:
  0.6 2.2 %copy-start = (bf16[128,16384]{1,0:T(8,128)(2,1)S(1)}, bf16[128,16384]{1,0:T(8,128)(2,1)}, u32[]{:S(2)}) copy-start(bf16[128,16384]{1,0:T(8,128)(2,1)} %states_ref.1) | copy-start | bytes 12582916
  2.8 0.8 copy-start.1
  3.7 0.8 copy-start.2

commit v3 on v2

--- a/solution.py
+++ b/solution.py
@@ -19,24 +19,91 @@
         ref[16 * r:16 * r + 16, :] = jnp.broadcast_to(values[r:r + 1, :], (16, LANES)).astype(ref.dtype)
 
 
-def local_tops(lw_t, bins_t):
-    rows = lw_t.shape[1]
-    tiles = BINS // LANES
+def sort_pairs(keys, values):
+    tile_bits = len(keys).bit_length() - 1
+    bits = tile_bits + 10
+    sub = lax.broadcasted_iota(jnp.int32, (8, LANES), 0)
     lane = lax.broadcasted_iota(jnp.int32, (8, LANES), 1)
 
-    def step(r, acc):
-        pick = jnp.full((LANES, LANES), r, jnp.int32)
-        col_w = jnp.take_along_axis(lw_t, pick, axis=1).reshape(LANES // 8, 8, LANES)
-        col_b = jnp.take_along_axis(bins_t, pick, axis=1).reshape(LANES // 8, 8, LANES)
-        out = []
-        for t in range(tiles):
-            member = col_b == (lane + t * LANES)[None]
-            out.append(jnp.maximum(acc[t], jnp.max(jnp.where(member, col_w, floor_value), axis=0)))
-        return tuple(out)
-
-    start = tuple(jnp.full((8, LANES), floor_value, jnp.float32) for _ in range(tiles))
-    acc = lax.fori_loop(0, rows, step, start)
-    return [jnp.max(a, axis=0, keepdims=True) for a in acc]
+    def mask_of(bit):
+        if bit < tile_bits + 3:
+            return (sub & (1 << (bit - tile_bits))) != 0
+        return (lane & (1 << (bit - tile_bits - 3))) != 0
+
+    def after(ka, va, kb, vb):
+        return (ka > kb) | ((ka == kb) & (va > vb))
+
+    for size in range(1, bits + 1):
+        for bit in range(size - 1, -1, -1):
+            down = mask_of(size) if tile_bits <= size < bits else None
+            if bit < tile_bits:
+                for t in range(len(keys)):
+                    o = t | (1 << bit)
+                    if o == t:
+                        continue
+                    swap = after(keys[t], values[t], keys[o], values[o])
+                    if down is not None:
+                        swap = jnp.logical_xor(swap, down)
+                    elif size < tile_bits and t & (1 << size):
+                        swap = after(keys[o], values[o], keys[t], values[t])
+                    keys[t], keys[o] = jnp.where(swap, keys[o], keys[t]), jnp.where(swap, keys[t], keys[o])
+                    values[t], values[o] = (jnp.where(swap, values[o], values[t]),
+                                            jnp.where(swap, values[t], values[o]))
+                continue
+            upper = mask_of(bit)
+            turn = upper if down is None else jnp.logical_xor(upper, down)
+            if bit < tile_bits + 3:
+                hop = 1 << (bit - tile_bits)
+
+                def partner(x):
+                    if 2 * hop == 8:
+                        return pltpu.roll(x, hop, 0)
+                    return jnp.where(upper, pltpu.roll(x, hop, 0), pltpu.roll(x, 8 - hop, 0))
+            else:
+                index = lane ^ (1 << (bit - tile_bits - 3))
+
+                def partner(x):
+                    return jnp.take_along_axis(x, index, axis=1)
+            for t in range(len(keys)):
+                k, v = partner(keys[t]), partner(values[t])
+                swap = jnp.logical_xor(after(keys[t], values[t], k, v), turn)
+                keys[t] = jnp.where(swap, k, keys[t])
+                values[t] = jnp.where(swap, v, values[t])
+    return keys, values
+
+
+def local_tops(lw, bins):
+    count = lw.shape[0] // 8
+    table = BINS // LANES
+    keys, values = sort_pairs([bins[8 * t:8 * t + 8] for t in range(count)],
+                              [lw[8 * t:8 * t + 8] for t in range(count)])
+    sub = lax.broadcasted_iota(jnp.int32, (8, LANES), 0)
+    lane = lax.broadcasted_iota(jnp.int32, (8, LANES), 1)
+    turned = pltpu.roll(keys[0], 7, 0)
+    following = jnp.where(sub == 7, pltpu.roll(turned, LANES - 1, 1), turned)
+    following = jnp.where((sub == 7) & (lane == LANES - 1), -1, following)
+    high_label = lax.broadcasted_iota(jnp.int32, (table, LANES), 0)
+    low_label = lax.broadcasted_iota(jnp.int32, (LANES, LANES), 0)
+    found = jnp.zeros((4 * table, LANES), jnp.float32)
+    for t in range(count):
+        last = keys[t] != (keys[t + 1] if t + 1 < count else following)
+        high = jnp.where(last, keys[t] // LANES, -1)
+        low = keys[t] % LANES
+        first = values[t].astype(jnp.bfloat16).astype(jnp.float32)
+        rest = values[t] - first
+        second = rest.astype(jnp.bfloat16).astype(jnp.float32)
+        third = rest - second
+        left, right = [], []
+        for r in range(8):
+            member = high[r:r + 1] == high_label
+            pieces = [jnp.where(member, x[r:r + 1], 0.0) for x in (first, second, third)]
+            pieces.append(jnp.where(member, 1.0, 0.0))
+            left.append(jnp.concatenate(pieces, axis=0).astype(jnp.bfloat16))
+            right.append(jnp.where(low[r:r + 1] == low_label, 1.0, 0.0).astype(jnp.bfloat16))
+        found = found + lax.dot_general(jnp.concatenate(left, axis=1), jnp.concatenate(right, axis=1),
+                                        (((1,), (1,)), ((), ())), preferred_element_type=jnp.float32)
+    top = (found[0:table] + found[table:2 * table]) + found[2 * table:3 * table]
+    return jnp.where(found[3 * table:] > 0.5, top, floor_value)
 
 
 def kernel(groups, whole_count, lw_ref, bins_ref, states_ref, cum_ref, means_ref, weights_ref,
@@ -66,13 +133,13 @@
     spread_rows(lo_b, (bins % width).astype(jnp.float32))
     spread_rows(hi_b, (bins // both).astype(jnp.float32))
     spread_rows(part_b, ((bins % both) // width).astype(jnp.float32))
-    tops = local_tops(lw.T, bins.T)
+    tops = local_tops(lw, bins)
     low, high = bins % LANES, bins // LANES
     own_top = jnp.zeros(lw.shape, jnp.float32)
     for t in range(BINS // LANES):
-        picked = jnp.take_along_axis(jnp.broadcast_to(tops[t], lw.shape), low, axis=1)
+        picked = jnp.take_along_axis(jnp.broadcast_to(tops[t:t + 1], lw.shape), low, axis=1)
         own_top = jnp.where(high == t, picked, own_top)
-        top_tab[t] = jnp.broadcast_to(tops[t], (8, LANES))
+        top_tab[t] = jnp.broadcast_to(tops[t:t + 1], (8, LANES))
     spread_rows(w_b, jnp.exp(lw - own_top))
     load.wait()
 

time: 102 us -> 60.1 us (0.59)
  Pallas kernels: 95.5 us -> 53.4 us
    pallas_call x1, Pallas kernels: 95.5 us -> 53.4 us  [body(): pl.pallas_call(functools.partial(kernel, groups, float(count * groups)),...]
where the time goes in v3:
time: 60.1 us; the launch traced here: 59.9 us
  Pallas kernels  53.4 us (89%)
  local copies, waits for them, and re-layouts  5.78 us (10%)
  between operations  0.65 us (1%)
    pallas_call x1, Pallas kernels, body(): pl.pallas_call(functools.partial(kernel, groups, float(count * groups)),...  53.4 us
    unnamed x9, local copies, waits for them, and re-layouts  5.78 us

profile of v3, /device:TPU:0, one launch (start us, length us, event | category | flops | bytes accessed | tf_op | source)
XLA Modules:
  0.0 59.9 jit_solution(18046915290388905106)
XLA Ops:
  0.6 0.0 copy-start
  0.6 2.2 %copy-done = bf16[128,16384]{1,0:T(8,128)(2,1)S(1)} copy-done((bf16[128,16384]{1,0:T(8,128)(2,1)S(1)}, bf16[128,16384]{1,0:T(8,128)(2,1)}, u32[]{:S(2)}) %copy-start) | copy-done | bytes 4194328
  2.8 0.0 copy-start.1
  2.8 0.8 %copy-done.1 = f32[16384]{0:T(1024)S(1)} copy-done((f32[16384]{0:T(1024)S(1)}, f32[16384]{0:T(1024)}, u32[]{:S(2)}) %copy-start.1) | copy-done | bytes 65560
  3.7 0.0 copy-start.2
  3.7 0.8 %copy-done.2 = s32[16384]{0:T(1024)S(1)} copy-done((s32[16384]{0:T(1024)S(1)}, s32[16384]{0:T(1024)}, u32[]{:S(2)}) %copy-start.2) | copy-done | bytes 65560
  4.5 53.4 %shard_map.58 = (f32[1,512]{1,0:T(1,128)S(1)}, f32[128,512]{1,0:T(8,128)S(1)}, f32[128,128]{1,0:T(8,128)S(1)}) custom-call(f32[128,128]{1,0:T(8,128)S(1)} %bitcast.4, s32[128,128]{1,0:T(8,128)S(1)} %bitcast.5, bf16[128,16384]{1,0:T(8,128)(2,1)S(1)} %copy-done), custom_call_target="tpu_custom_call" | custom-call | tf_op jit(solution)/shard_map/pallas_call | solution.py:290
  57.9 0.6 copy.9
  58.5 0.7 %copy.10 = f32[128,512]{1,0:T(8,128)} copy(f32[128,512]{1,0:T(8,128)S(1)} %get-tuple-element.13) | data formatting | bytes 524288
  59.2 0.6 %copy.11 = f32[16384]{0:T(1024)} copy(f32[16384]{0:T(1024)S(1)} %bitcast.6) | data formatting | bytes 131072
Async XLA Ops:
  0.6 2.2 %copy-start = (bf16[128,16384]{1,0:T(8,128)(2,1)S(1)}, bf16[128,16384]{1,0:T(8,128)(2,1)}, u32[]{:S(2)}) copy-start(bf16[128,16384]{1,0:T(8,128)(2,1)} %states_ref.1) | copy-start | bytes 12582916
  2.8 0.8 %copy-start.1 = (f32[16384]{0:T(1024)S(1)}, f32[16384]{0:T(1024)}, u32[]{:S(2)}) copy-start(f32[16384]{0:T(1024)} %param.3) | copy-start | bytes 196612
  3.7 0.8 %copy-start.2 = (s32[16384]{0:T(1024)S(1)}, s32[16384]{0:T(1024)}, u32[]{:S(2)}) copy-start(s32[16384]{0:T(1024)} %param.4) | copy-start | bytes 196612

commit v4 on v3

--- a/solution.py
+++ b/solution.py
@@ -207,8 +207,8 @@
             lanes = slice(p * width, (p + 1) * width)
             sums, mass = part_of(found, 1 - core, p)
             pair_send[s, 0:state, lanes] = sums
-            pair_send[s, state:state + 8, lanes] = jnp.broadcast_to(mass, (8, width))
-            pair_send[s, state + 8:state + 16, lanes] = tops_of(dest * 2 + 1 - core, p)
+            pair_send[s, state:state + 4, lanes] = jnp.broadcast_to(mass, (4, width))
+            pair_send[s, state + 4:state + 8, lanes] = tops_of(dest * 2 + 1 - core, p)[0:4]
         copy = pltpu.make_async_remote_copy(
             pair_send.at[s], pair_recv.at[s], pair_ss.at[s], pair_rs.at[s],
             device_id={"dom": partner}, device_id_type=pl.DeviceIdType.MESH)
@@ -218,13 +218,13 @@
         for p in range(half):
             lanes = slice(p * width, (p + 1) * width)
             sums, mass = part_of(found, core, p)
-            mine = tops_of(dest * 2 + core, p)
-            theirs = pair_recv[s, state + 8:state + 16, lanes]
+            mine = tops_of(dest * 2 + core, p)[0:4]
+            theirs = pair_recv[s, state + 4:state + 8, lanes]
             top = jnp.maximum(mine, theirs)
             by_mine, by_theirs = jnp.exp(mine - top), jnp.exp(theirs - top)
             chip_send[s, 0:state, lanes] = sums * by_mine[0:1] + pair_recv[s, 0:state, lanes] * by_theirs[0:1]
-            chip_send[s, state:state + 8, lanes] = mass * by_mine + pair_recv[s, state:state + 8, lanes] * by_theirs
-            chip_send[s, state + 8:state + 16, lanes] = top
+            chip_send[s, state:state + 4, lanes] = mass * by_mine + pair_recv[s, state:state + 4, lanes] * by_theirs
+            chip_send[s, state + 4:state + 8, lanes] = top
         if m:
             copy = pltpu.make_async_remote_copy(
                 chip_send.at[s], chip_recv.at[s], chip_ss.at[s], chip_rs.at[s],
@@ -235,7 +235,7 @@
     for copy in chip_copies:
         copy.wait_recv()
     last = chips - 1
-    tops = [chip_send[last, state + 8:state + 9, :]] + [chip_recv[s, state + 8:state + 9, :] for s in range(last)]
+    tops = [chip_send[last, state + 4:state + 5, :]] + [chip_recv[s, state + 4:state + 5, :] for s in range(last)]
     bin_top = functools.reduce(jnp.maximum, tops)
     sums = chip_send[last, 0:state + 8, :] * jnp.exp(tops[0] - bin_top)
     for s in range(last):
@@ -286,7 +286,7 @@
     width = min(256, owned)
     split = 2 * owned // width
     vmem = pl.BlockSpec(memory_space=pltpu.VMEM)
-    blocks = pltpu.VMEM((chips, state + EXTRA, owned), jnp.float32)
+    blocks = pltpu.VMEM((chips, state + 8, owned), jnp.float32)
     cumulative, bin_means, weights = pl.pallas_call(
         functools.partial(kernel, groups, float(count * groups)),
         out_shape=(jax.ShapeDtypeStruct((1, owned), jnp.float32),

time: 60.1 us -> 58.7 us (0.977)
  Pallas kernels: 53.4 us -> 52 us
    pallas_call x1, Pallas kernels: 53.4 us -> 52 us  [body(): pl.pallas_call(functools.partial(kernel, groups, float(count * groups)),...]
where the time goes in v4:
time: 58.7 us; the launch traced here: 58.4 us
  Pallas kernels  52 us (89%)
  local copies, waits for them, and re-layouts  5.78 us (10%)
  between operations  0.65 us (1%)
    pallas_call x1, Pallas kernels, body(): pl.pallas_call(functools.partial(kernel, groups, float(count * groups)),...  52 us
    unnamed x9, local copies, waits for them, and re-layouts  5.78 us

profile of v4, /device:TPU:0, one launch (start us, length us, event | category | flops | bytes accessed | tf_op | source)
XLA Modules:
  0.0 58.4 jit_solution(4873651472019787522)
XLA Ops:
  0.6 0.0 copy-start
  0.6 2.2 %copy-done = bf16[128,16384]{1,0:T(8,128)(2,1)S(1)} copy-done((bf16[128,16384]{1,0:T(8,128)(2,1)S(1)}, bf16[128,16384]{1,0:T(8,128)(2,1)}, u32[]{:S(2)}) %copy-start) | copy-done | bytes 4194328
  2.8 0.0 copy-start.1
  2.8 0.8 %copy-done.1 = f32[16384]{0:T(1024)S(1)} copy-done((f32[16384]{0:T(1024)S(1)}, f32[16384]{0:T(1024)}, u32[]{:S(2)}) %copy-start.1) | copy-done | bytes 65560
  3.7 0.0 copy-start.2
  3.7 0.8 %copy-done.2 = s32[16384]{0:T(1024)S(1)} copy-done((s32[16384]{0:T(1024)S(1)}, s32[16384]{0:T(1024)}, u32[]{:S(2)}) %copy-start.2) | copy-done | bytes 65560
  4.5 52.0 %shard_map.58 = (f32[1,512]{1,0:T(1,128)S(1)}, f32[128,512]{1,0:T(8,128)S(1)}, f32[128,128]{1,0:T(8,128)S(1)}) custom-call(f32[128,128]{1,0:T(8,128)S(1)} %bitcast.4, s32[128,128]{1,0:T(8,128)S(1)} %bitcast.5, bf16[128,16384]{1,0:T(8,128)(2,1)S(1)} %copy-done), custom_call_target="tpu_custom_call" | custom-call | tf_op jit(solution)/shard_map/pallas_call | solution.py:290
  56.5 0.6 copy.9
  57.1 0.7 %copy.10 = f32[128,512]{1,0:T(8,128)} copy(f32[128,512]{1,0:T(8,128)S(1)} %get-tuple-element.13) | data formatting | bytes 524288
  57.8 0.6 %copy.11 = f32[16384]{0:T(1024)} copy(f32[16384]{0:T(1024)S(1)} %bitcast.6) | data formatting | bytes 131072
Async XLA Ops:
  0.6 2.2 %copy-start = (bf16[128,16384]{1,0:T(8,128)(2,1)S(1)}, bf16[128,16384]{1,0:T(8,128)(2,1)}, u32[]{:S(2)}) copy-start(bf16[128,16384]{1,0:T(8,128)(2,1)} %states_ref.1) | copy-start | bytes 12582916
  2.8 0.8 %copy-start.1 = (f32[16384]{0:T(1024)S(1)}, f32[16384]{0:T(1024)}, u32[]{:S(2)}) copy-start(f32[16384]{0:T(1024)} %param.3) | copy-start | bytes 196612
  3.7 0.8 %copy-start.2 = (s32[16384]{0:T(1024)S(1)}, s32[16384]{0:T(1024)}, u32[]{:S(2)}) copy-start(s32[16384]{0:T(1024)} %param.4) | copy-start | bytes 196612
